TPU v7x, 8 devices: a whole 2x2x1 slice. The times are simulated.
8 devices in a mesh: dp: 1 (over z), ri: 2 (over y), co: 2 (over x), ro: 2 (over core).
Axes of the slice: x: 2, y: 2, z: 1, core: 2. Of those that a mesh axis runs over, the one named last changes fastest.
Arguments:
- a_mat: bfloat16 [5120, 32768], P(('dp', 'ri', 'ro'), 'co')
- b_mat: bfloat16 [32768, 13824], P(('dp', 'ri', 'ro'), 'co')
Outputs:
- output: bfloat16 [5120, 13824], P(('dp', 'ri', 'ro'), 'co')
All inputs are finite; a program needn't handle non-finite values.
Results may differ from a plain program's by a relative error of at most 0.001.
Values are sent between devices in bfloat16 or wider.
A program may use at most 1 GiB of HBM per device.

v0:
```python
import jax
import jax.numpy as jnp
from jax import lax
from jax.sharding import PartitionSpec as P, NamedSharding


def solution(mesh):
    grid_spec = P(("dp", "ri", "ro"), "co")

    def local_block(a_block, b_block):
        a_rows = lax.all_gather(a_block, "co", axis=1, tiled=True)
        b_cols = lax.all_gather(b_block, ("ri", "ro"), axis=0, tiled=True)
        product = jnp.dot(a_rows, b_cols, preferred_element_type=jnp.float32)
        return product.astype(jnp.bfloat16)

    return jax.shard_map(local_block, mesh=mesh, in_specs=(grid_spec, grid_spec), out_specs=grid_spec, check_vma=False)
```

profile of v0, /device:TPU:0, one launch (start us, length us, event | category | flops | bytes accessed | tf_op | source)
XLA Modules:
  0.0 4155.8 jit_solution(16622229744718980437)
XLA Ops:
  6.5 0.0 all-gather.3.cloned.1.call-start
  6.5 0.7 all-gather.3.cloned.1.call-update
  7.3 0.0 all-gather.5.cloned.1.call-start
  7.3 0.7 all-gather.5.cloned.1.call-update
  8.0 955.7 %all-gather.3.cloned.1.call-done = bf16[1280,32768]{1,0:T(8,128)(2,1)} async-done(((bf16[1280,16384]{1,0:T(8,128)(2,1)}), bf16[1280,32768]{1,0:T(8,128)(2,1)}) %all-gather.3.cloned.1.call-update) | async-done | bytes 83886096 | tf_op jit(solution)/shard_map/all_gather | solution.py:11
  963.7 2580.0 %all-gather.5.cloned.1.call-done = bf16[32768,6912]{1,0:T(8,128)(2,1)} async-done(((bf16[8192,6912]{1,0:T(8,128)(2,1)}), bf16[32768,6912]{1,0:T(8,128)(2,1)}) %all-gather.5.cloned.1.call-update) | async-done | bytes 452984832 | tf_op jit(solution)/shard_map/all_gather | solution.py:12
  3543.6 605.3 %convolution_convert_fusion = bf16[1280,6912]{1,0:T(8,128)(2,1)} fusion(bf16[1280,32768]{1,0:T(8,128)(2,1)} %all-gather.3.cloned.1.call-done, bf16[32768,6912]{1,0:T(8,128)(2,1)} %all-gather.5.cloned.1.call-done), kind=kOutput, calls=%fused_computation | convolution fusion | flops 579829432320 | bytes 554565632 | tf_op jit(solution)/shard_map/dot_general | solution.py:13
Async XLA Ops:
  6.5 957.2 %all-gather.3.cloned.1.call-start = ((), (), s32[]{:S(2)}) async-start(), calls=%async_computation | async-start | bytes 125829120 | tf_op jit(solution)/shard_map/all_gather | solution.py:11
  7.3 3536.4 %all-gather.5.cloned.1.call-start = ((), (), s32[]{:S(2)}) async-start(), calls=%async_computation.1 | async-start | bytes 566231040 | tf_op jit(solution)/shard_map/all_gather | solution.py:12
Sparse Core Ops, SparseCore 0:
  8.8 954.7 all-gather.2
  965.2 2578.3 all-gather.4
where the time goes:
time: 4160 us
  waiting for transfers between devices  3540 us (85%)
  matrix products  605 us (15%)
    all_gather x1, waiting for transfers between devices, local_block(): b_cols = lax.all_gather(b_block, ('ri', 'ro'), axis=0, tiled=True)  2580 us
    all_gather x1, waiting for transfers between devices, local_block(): a_rows = lax.all_gather(a_block, 'co', axis=1, tiled=True)  956 us
    dot_general x1, matrix products, local_block(): product = jnp.dot(a_rows, b_cols, preferred_element_type=jnp.float32)  605 us
  transfers between devices with their start and end apart: 2, of which 2 were waited for; matrix products, arithmetic and copies ran while one was open for 0% of the time, Pallas kernels for 0%

commit v1 on v0

v1 whole, which is shorter than its diff:
```python
import functools

import jax
import jax.numpy as jnp
from jax import lax
from jax.experimental import pallas as pl
from jax.experimental.pallas import tpu as pltpu
from jax.sharding import PartitionSpec as P

MESH = pl.DeviceIdType.MESH
PIECES = 16
EXTRA = 64


def _kernel(extra, tile, out_tile, a_ref, b_ref, c_ref, z_ref, x_ref, t_ref, bs_ref, ps_ref, pr_ref,
            acc, av, bv, prv, ov, zf_recv, zg_recv, t_recv, x_recv, b_recv, c_recv,
            y_send, f_send, x_send, b_send, c_send, a_sem, b_sem, p_sem, pr_sem, o_sem):
    ri, co, ro = lax.axis_index("ri"), lax.axis_index("co"), lax.axis_index("ro")
    diag = ri == co
    far = ri != co
    x_dev, y_dev, sib = {"co": 1 - co}, {"ri": 1 - ri}, {"ro": 1 - ro}

    half = a_ref.shape[0] // 2
    kt = a_ref.shape[1] // PIECES
    cols = b_ref.shape[1]
    own = PIECES // 2
    steps = 4 * PIECES
    f = jnp.where(diag, 0, half)
    g = half - f

    def kcols(j):
        return pl.ds(pl.multiple_of(lax.rem(j + own * ro, PIECES) * kt, kt), kt)

    def rows(base, n):
        return pl.ds(pl.multiple_of(base, 16), n)

    def remote(src, dst, send, recv, dev):
        return pltpu.make_async_remote_copy(src_ref=src, dst_ref=dst, send_sem=send, recv_sem=recv,
                                            device_id=dev, device_id_type=MESH)

    relay_rows = half + extra

    def first_y(j):
        return remote(a_ref.at[pl.ds(0, half), kcols(j)], z_ref.at[pl.ds(0, half), kcols(j)],
                      y_send, zf_recv.at[j], y_dev)

    def first_x(j):
        return remote(a_ref.at[pl.ds(half - extra, relay_rows), kcols(j)], t_ref.at[:, kcols(j)],
                      x_send, t_recv.at[j], x_dev)

    def relay(j):
        return remote(t_ref.at[:, kcols(j)], z_ref.at[pl.ds(half - extra, relay_rows), kcols(j)],
                      y_send, zf_recv.at[j], y_dev)

    def pass_diag(j):
        r = pl.ds(0, half - extra)
        return remote(z_ref.at[r, kcols(j)], z_ref.at[r, kcols(j)], f_send, zg_recv.at[j], x_dev)

    def pass_far(j):
        r = pl.ds(half, half)
        return remote(z_ref.at[r, kcols(j)], z_ref.at[r, kcols(j)], f_send, zg_recv.at[j], x_dev)

    def give_x(q):
        blk, j = q // PIECES, lax.rem(q, PIECES)
        at = (rows(blk * half, half), kcols(j))
        return remote(a_ref.at[at], x_ref.at[at], x_send, x_recv.at[q], x_dev)

    def give_b(i):
        r = rows(i * kt, kt)
        return remote(b_ref.at[r], bs_ref.at[r], b_send.at[i], b_recv.at[i], sib)

    def give_c(blk):
        r = rows(jnp.where(blk == 0, f, g), half)
        return remote(ps_ref.at[r], pr_ref.at[r], c_send.at[blk], c_recv.at[blk], y_dev)

    def base_of(blk):
        return jnp.where((blk == 0) | (blk == 3), f, g)

    def load_a(src, s):
        blk, j, slot = s // PIECES, lax.rem(s, PIECES), lax.rem(s, 2)
        return pltpu.make_async_copy(src.at[rows(base_of(blk), half), kcols(j)], av.at[slot], a_sem.at[slot])

    def load_b(src, i, s):
        slot = lax.rem(s, 2)
        return pltpu.make_async_copy(src.at[rows(i * kt, kt)], bv.at[slot], b_sem.at[slot])

    def start_b(s):
        blk, j = s // PIECES, lax.rem(s, PIECES)

        @pl.when(j < own)
        def _():
            load_b(b_ref, j, s).start()

        @pl.when(j >= own)
        def _():
            @pl.when(blk == 0)
            def _():
                give_b(j - own).wait_recv()
            load_b(bs_ref, j - own, s).start()

    barrier = pltpu.get_barrier_semaphore()
    for dev in (x_dev, y_dev, sib):
        pl.semaphore_signal(barrier, inc=1, device_id=dev, device_id_type=MESH)
    pl.semaphore_wait(barrier, 3)

    @pl.when(far)
    def _():
        def go(j, carry):
            first_x(j).start()
            first_y(j).start()
            return carry
        lax.fori_loop(0, PIECES, go, 0)

    @pl.when(diag)
    def _():
        give_x(0).start()
        give_x(1).start()

    def go_b(i, carry):
        give_b(i).start()
        return carry
    lax.fori_loop(0, own, go_b, 0)
    start_b(0)

    def step(s, carry):
        blk, j, slot = s // PIECES, lax.rem(s, PIECES), lax.rem(s, 2)

        @pl.when(s + 1 < steps)
        def _():
            start_b(s + 1)

        @pl.when(blk == 0)
        def _():
            @pl.when(diag)
            def _():
                first_y(j).wait_recv()
                pass_diag(j).start()
                load_a(z_ref, s).start()
                first_x(j).wait_recv()
                relay(j).start()

            @pl.when(far)
            def _():
                relay(j).wait_recv()
                pass_far(j).start()
                load_a(z_ref, s).start()

        @pl.when((s == PIECES - 1) & diag)
        def _():
            def go(q, carry):
                give_x(q).start()
                return carry
            lax.fori_loop(2, 2 * PIECES, go, 0)

        @pl.when(blk == 1)
        def _():
            @pl.when(diag)
            def _():
                pass_far(j).wait_recv()

            @pl.when(far)
            def _():
                pass_diag(j).wait_recv()
            load_a(z_ref, s).start()

        @pl.when((blk >= 2) & far)
        def _():
            give_x(s - 2 * PIECES).wait_recv()
            load_a(x_ref, s).start()

        load_a(a_ref, s).wait()

        @pl.when((s + 1 >= 2 * PIECES) & (s + 1 < steps) & diag)
        def _():
            load_a(a_ref, s + 1).start()

        load_b(b_ref, 0, s).wait()

        @pl.when(j == 0)
        def _():
            def body(n, carry):
                cs = pl.ds(pl.multiple_of(n * tile, tile), tile)
                acc[:, cs] = jnp.dot(av[slot], bv[slot, :, cs], preferred_element_type=jnp.float32)
                return carry
            lax.fori_loop(0, cols // tile, body, 0)

        @pl.when(j > 0)
        def _():
            def body(n, carry):
                cs = pl.ds(pl.multiple_of(n * tile, tile), tile)
                acc[:, cs] += jnp.dot(av[slot], bv[slot, :, cs], preferred_element_type=jnp.float32)
                return carry
            lax.fori_loop(0, cols // tile, body, 0)

        @pl.when((j == PIECES - 1) & (blk < 2))
        def _():
            store = pltpu.make_async_copy(acc, ps_ref.at[rows(base_of(blk), half)], p_sem)
            store.start()
            store.wait()
            give_c(blk).start()

        @pl.when((j == PIECES - 1) & (blk >= 2))
        def _():
            base = base_of(blk)
            give_c(blk - 2).wait_recv()
            n_out = cols // out_tile

            def part(n):
                return pl.ds(pl.multiple_of(n * out_tile, out_tile), out_tile)

            def fetch(n):
                at = lax.rem(n, 2)
                return pltpu.make_async_copy(pr_ref.at[rows(base, half), part(n)], prv.at[at], pr_sem.at[at])

            def put(n):
                at = lax.rem(n, 2)
                return pltpu.make_async_copy(ov.at[at], c_ref.at[rows(base, half), part(n)], o_sem.at[at])

            fetch(0).start()

            def finish(n, carry):
                at = lax.rem(n, 2)

                @pl.when(n + 1 < n_out)
                def _():
                    fetch(n + 1).start()
                fetch(n).wait()

                @pl.when(n >= 2)
                def _():
                    put(n - 2).wait()
                ov[at] = (acc[:, part(n)] + prv[at]).astype(ov.dtype)
                put(n).start()
                return carry
            lax.fori_loop(0, n_out, finish, 0)

            @pl.when(n_out >= 2)
            def _():
                put(n_out - 2).wait()
            put(n_out - 1).wait()
        return carry

    lax.fori_loop(0, steps, step, 0)

    def sent(src, sem):
        pltpu.make_async_remote_copy(src_ref=src, dst_ref=src, send_sem=sem, recv_sem=zf_recv.at[0],
                                     device_id=x_dev, device_id_type=MESH).wait_send()

    @pl.when(diag)
    def _():
        sent(t_ref, y_send)
        sent(z_ref.at[pl.ds(0, half - extra)], f_send)
        sent(a_ref, x_send)

    @pl.when(far)
    def _():
        sent(a_ref.at[pl.ds(0, half)], y_send)
        sent(z_ref.at[pl.ds(half, half)], f_send)
        sent(a_ref.at[pl.ds(half - extra, relay_rows)], x_send)

    def done_b(i, carry):
        give_b(i).wait_send()
        return carry
    lax.fori_loop(0, own, done_b, 0)
    give_c(0).wait_send()
    give_c(1).wait_send()


def solution(mesh, extra=EXTRA, tile=256, out_tile=768):
    grid_spec = P(("dp", "ri", "ro"), "co")

    def local_block(a_block, b_block):
        m, k = a_block.shape
        depth, n = b_block.shape
        half, kt = m // 2, k // PIECES
        bf16, f32 = jnp.bfloat16, jnp.float32
        hbm = pl.BlockSpec(memory_space=pl.ANY)
        dma = pltpu.SemaphoreType.DMA
        outs = pl.pallas_call(
            functools.partial(_kernel, extra, tile, out_tile),
            out_shape=[
                jax.ShapeDtypeStruct((m, n), bf16),
                jax.ShapeDtypeStruct((m, k), bf16),
                jax.ShapeDtypeStruct((m, k), bf16),
                jax.ShapeDtypeStruct((half + extra, k), bf16),
                jax.ShapeDtypeStruct((depth, n), bf16),
                jax.ShapeDtypeStruct((m, n), f32),
                jax.ShapeDtypeStruct((m, n), f32),
            ],
            in_specs=[hbm, hbm],
            out_specs=[hbm] * 7,
            scratch_shapes=[
                pltpu.VMEM((half, n), f32),
                pltpu.VMEM((2, half, kt), bf16),
                pltpu.VMEM((2, kt, n), bf16),
                pltpu.VMEM((2, half, out_tile), f32),
                pltpu.VMEM((2, half, out_tile), bf16),
                dma((PIECES,)), dma((PIECES,)), dma((PIECES,)), dma((2 * PIECES,)),
                dma((PIECES // 2,)), dma((2,)),
                dma, dma, dma, dma((PIECES // 2,)), dma((2,)),
                dma((2,)), dma((2,)), dma, dma((2,)), dma((2,)),
            ],
            compiler_params=pltpu.CompilerParams(
                collective_id=0, has_side_effects=True, vmem_limit_bytes=63_000_000),
        )(a_block, b_block)
        return outs[0]

    return jax.shard_map(local_block, mesh=mesh, in_specs=(grid_spec, grid_spec), out_specs=grid_spec, check_vma=False)
```

time: 4160 us -> 1530 us (0.37)
  the two profiles are of different devices: /device:TPU:0 before, /device:TPU:2 now
where the time goes in v1:
time: 1530 us; the launch traced here: 1520 us
  Pallas kernels  1510 us (99%)
  local copies, waits for them, and re-layouts  15.7 us (1%)
    pallas_call x1, Pallas kernels, local_block(): pl.pallas_call(functools.partial(_kernel, extra, tile, out_tile), out_sha...  1510 us

profile of v1, /device:TPU:2, one launch (start us, length us, event | category | flops | bytes accessed | tf_op | source)
XLA Modules:
  0.0 1524.4 jit_solution(14216750261041033068)
XLA Ops:
  0.0 1508.6 %shard_map.28 = (bf16[1280,6912]{1,0:T(8,128)(2,1)}, bf16[1280,16384]{1,0:T(8,128)(2,1)}, bf16[1280,16384]{1,0:T(8,128)(2,1)}, bf16[704,16384]{1,0:T(8,128)(2,1)...) custom-call(bf16[1280,16384]{1,0:T(8,128)(2,1)} %a_ref.1, bf16[8192,6912]{1,0:T(8,128)(2,1)} %b_ref.1), custom_call_target="tpu_custom_call" | custom-call | tf_op jit(solution)/shard_map/pallas_call | solution.py:279
  1508.6 15.7 %copy.4 = bf16[1280,6912]{1,0:T(8,128)(2,1)} copy(bf16[1280,6912]{1,0:T(8,128)(2,1)} %get-tuple-element.6) | data formatting | bytes 35389440

commit v2 on v0

v2 whole, which is shorter than its diff:
```python
import functools

import jax
import jax.numpy as jnp
from jax import lax
from jax.experimental import pallas as pl
from jax.experimental.pallas import tpu as pltpu
from jax.sharding import PartitionSpec as P

MESH = pl.DeviceIdType.MESH
PIECES = 16
EXTRA = 80
AHEAD = 8


def _kernel(extra, tile, out_tile, a_ref, b_ref, c_ref, z_ref, x_ref, t_ref, bs_ref, ps_ref, pr_ref,
            acc, zacc, av, bv, prv, ov, zf_recv, zg_recv, t_recv, x_recv, b_recv, c_recv,
            y_send, f_send, x_send, b_send, c_send, a_sem, b_sem, p_sem, pr_sem, o_sem):
    ri, co, ro = lax.axis_index("ri"), lax.axis_index("co"), lax.axis_index("ro")
    diag = ri == co
    far = ri != co
    x_dev, y_dev, sib = {"co": 1 - co}, {"ri": 1 - ri}, {"ro": 1 - ro}

    half = a_ref.shape[0] // 2
    quart = half // 2
    kt = a_ref.shape[1] // PIECES
    cols = b_ref.shape[1]
    own = PIECES // 2
    f = jnp.where(diag, 0, half)
    g = half - f

    def kcols(j):
        return pl.ds(pl.multiple_of(lax.rem(j + own * ro, PIECES) * kt, kt), kt)

    def rows(base, n):
        return pl.ds(pl.multiple_of(base, 8), n)

    def f_rows(h):
        return rows(jnp.where(diag, h, 3 - h) * quart, quart)

    def g_rows(h):
        return rows(jnp.where(diag, 3 - h, h) * quart, quart)

    def remote(src, dst, send, recv, dev):
        return pltpu.make_async_remote_copy(src_ref=src, dst_ref=dst, send_sem=send, recv_sem=recv,
                                            device_id=dev, device_id_type=MESH)

    def t_rows(h):
        return pl.ds(3 * quart, quart) if h == 0 else pl.ds(half - extra, quart + extra)

    def t_at(h):
        return pl.ds(quart + extra, quart) if h == 0 else pl.ds(0, quart + extra)

    def d_rows(h):
        return pl.ds(0, quart) if h == 0 else pl.ds(quart, quart - extra)

    def first_y(h, j):
        r = pl.ds(h * quart, quart)
        return remote(a_ref.at[r, kcols(j)], z_ref.at[r, kcols(j)], y_send, zf_recv.at[h, j], y_dev)

    def first_x(h, j):
        return remote(a_ref.at[t_rows(h), kcols(j)], t_ref.at[t_at(h), kcols(j)], x_send, t_recv.at[h, j], x_dev)

    def relay(h, j):
        return remote(t_ref.at[t_at(h), kcols(j)], z_ref.at[t_rows(h), kcols(j)], y_send, zf_recv.at[h, j], y_dev)

    def pass_diag(h, j):
        at = (d_rows(h), kcols(j))
        return remote(z_ref.at[at], z_ref.at[at], f_send, zg_recv.at[h, j], x_dev)

    def pass_far(h, j):
        at = (pl.ds((3 - h) * quart, quart), kcols(j))
        return remote(z_ref.at[at], z_ref.at[at], f_send, zg_recv.at[h, j], x_dev)

    def give_x(q):
        at = (rows(q // PIECES * half, half), kcols(lax.rem(q, PIECES)))
        return remote(a_ref.at[at], x_ref.at[at], x_send, x_recv.at[q], x_dev)

    def give_b(i):
        r = rows(i * kt, kt)
        return remote(b_ref.at[r], bs_ref.at[r], b_send.at[i], b_recv.at[i], sib)

    def give_c(q):
        r = (f_rows if q < 2 else g_rows)(q % 2)
        return remote(ps_ref.at[r], pr_ref.at[r], c_send.at[q], c_recv.at[q], y_dev)

    def load_a(src, r, j):
        slot = lax.rem(j, 2)
        n = quart if r.size == quart else half
        return pltpu.make_async_copy(src.at[r, kcols(j)], av.at[slot, pl.ds(0, n)], a_sem.at[slot])

    def start_b(j, fresh=False):
        slot = lax.rem(j, 2)

        @pl.when(j < own)
        def _():
            pltpu.make_async_copy(b_ref.at[rows(j * kt, kt)], bv.at[slot], b_sem.at[slot]).start()

        @pl.when(j >= own)
        def _():
            if fresh:
                give_b(j - own).wait_recv()
            pltpu.make_async_copy(bs_ref.at[rows((j - own) * kt, kt)], bv.at[slot], b_sem.at[slot]).start()

    def wait_b(j):
        slot = lax.rem(j, 2)
        pltpu.make_async_copy(b_ref.at[rows(0, kt)], bv.at[slot], b_sem.at[slot]).wait()

    def next_b(j, fresh=False, last=False):
        if last:
            @pl.when(j + 1 < PIECES)
            def _():
                start_b(j + 1)
        else:
            start_b(lax.rem(j + 1, PIECES), fresh)

    def multiply(total, n, j):
        slot = lax.rem(j, 2)

        def product(i):
            cs = pl.ds(pl.multiple_of(i * tile, tile), tile)
            return cs, jnp.dot(av[slot, :n], bv[slot, :, cs], preferred_element_type=jnp.float32)

        @pl.when(j == 0)
        def _():
            def body(i, carry):
                cs, part = product(i)
                total[:, cs] = part
                return carry
            lax.fori_loop(0, cols // tile, body, 0)

        @pl.when(j > 0)
        def _():
            def body(i, carry):
                cs, part = product(i)
                total[:, cs] += part
                return carry
            lax.fori_loop(0, cols // tile, body, 0)

    def store_total(r):
        store = pltpu.make_async_copy(zacc, ps_ref.at[r], p_sem)
        store.start()
        store.wait()

    n_out = cols // out_tile

    def finish(base, from_step):
        def part(n):
            return pl.ds(pl.multiple_of(n * out_tile, out_tile), out_tile)

        def fetch(n):
            at = lax.rem(n, 2)
            return pltpu.make_async_copy(pr_ref.at[rows(base, half), part(n)], prv.at[at], pr_sem.at[at])

        def put(n):
            at = lax.rem(n, 2)
            return pltpu.make_async_copy(ov.at[at], c_ref.at[rows(base, half), part(n)], o_sem.at[at])

        fetch(0).start()

        def body(n, carry):
            at = lax.rem(n, 2)

            @pl.when(n + 1 < n_out)
            def _():
                fetch(n + 1).start()
            fetch(n).wait()

            @pl.when(n >= 2)
            def _():
                put(n - 2).wait()
            for i in range(out_tile // tile):
                ts = pl.ds(i * tile, tile)
                cs = pl.ds(pl.multiple_of(n * out_tile + i * tile, tile), tile)
                total = acc[:, cs] + prv[at, :, ts]
                if from_step:
                    total += jnp.dot(av[(PIECES - 1) % 2], bv[(PIECES - 1) % 2, :, cs],
                                     preferred_element_type=jnp.float32)
                ov[at, :, ts] = total.astype(ov.dtype)
            put(n).start()
            return carry
        lax.fori_loop(0, n_out, body, 0)
        if n_out >= 2:
            put(n_out - 2).wait()
        put(n_out - 1).wait()

    barrier = pltpu.get_barrier_semaphore()
    for dev in (x_dev, y_dev, sib):
        pl.semaphore_signal(barrier, inc=1, device_id=dev, device_id_type=MESH)
    pl.semaphore_wait(barrier, 3)

    @pl.when(far)
    def _():
        for h in range(2):
            def go(j, carry):
                first_x(h, j).start()
                first_y(h, j).start()
                return carry
            lax.fori_loop(0, PIECES, go, 0)

    def go_x(q, carry):
        give_x(q).start()
        return carry

    @pl.when(diag)
    def _():
        lax.fori_loop(0, AHEAD, go_x, 0)

    def go_b(i, carry):
        give_b(i).start()
        return carry
    lax.fori_loop(0, own, go_b, 0)
    start_b(0)

    for h in range(2):
        def f_step(j, carry):
            next_b(j, fresh=h == 0)

            @pl.when(diag)
            def _():
                with jax.named_scope("wait_zf_diag"):
                    first_y(h, j).wait_recv()
                pass_diag(h, j).start()
                load_a(z_ref, f_rows(h), j).start()
                with jax.named_scope("wait_t"):
                    first_x(h, j).wait_recv()
                relay(h, j).start()

            @pl.when(far)
            def _():
                with jax.named_scope("wait_zf_far"):
                    relay(h, j).wait_recv()
                pass_far(h, j).start()
                load_a(z_ref, f_rows(h), j).start()
            load_a(z_ref, f_rows(h), j).wait()
            with jax.named_scope("wait_b"):
                wait_b(j)
            multiply(zacc, quart, j)
            return carry
        lax.fori_loop(0, PIECES, f_step, 0)

        if h == 1:
            @pl.when(diag)
            def _():
                lax.fori_loop(AHEAD, 2 * PIECES, go_x, 0)
        store_total(f_rows(h))
    give_c(0).start()
    give_c(1).start()

    def x_block(blk, base, diag_branch, last):
        src = a_ref if diag_branch else x_ref

        def x_step(j, carry):
            next_b(j, last=last)
            if diag_branch:
                load_a(src, rows(base, half), j).start()
            else:
                with jax.named_scope("wait_x"):
                    give_x(blk * PIECES + j).wait_recv()
                load_a(src, rows(base, half), j).start()
            load_a(src, rows(base, half), j).wait()
            wait_b(j)

            if last:
                @pl.when(j < PIECES - 1)
                def _():
                    multiply(acc, half, j)
            else:
                multiply(acc, half, j)
            return carry
        lax.fori_loop(0, PIECES, x_step, 0)

    @pl.when(diag)
    def _():
        with jax.named_scope("xg_diag"):
            x_block(0, g, True, False)

    for h in range(2):
        def g_step(j, carry):
            next_b(j)

            @pl.when(diag)
            def _():
                with jax.named_scope("wait_zg_diag"):
                    pass_far(h, j).wait_recv()

            @pl.when(far)
            def _():
                with jax.named_scope("wait_zg_far"):
                    pass_diag(h, j).wait_recv()
            load_a(z_ref, g_rows(h), j).start()
            load_a(z_ref, g_rows(h), j).wait()
            wait_b(j)
            multiply(zacc, quart, j)
            return carry
        lax.fori_loop(0, PIECES, g_step, 0)
        store_total(g_rows(h))
        give_c(2 + h).start()

    @pl.when(far)
    def _():
        with jax.named_scope("xg_far"):
            x_block(0, g, False, False)

    with jax.named_scope("wait_c_first"):
        give_c(0).wait_recv()
        give_c(1).wait_recv()
    with jax.named_scope("finish_first"):
        finish(g, False)

    @pl.when(diag)
    def _():
        x_block(1, f, True, True)

    @pl.when(far)
    def _():
        x_block(1, f, False, True)

    with jax.named_scope("wait_c_last"):
        give_c(2).wait_recv()
        give_c(3).wait_recv()
    with jax.named_scope("finish_last"):
        finish(f, True)

    def sent(src, sem):
        pltpu.make_async_remote_copy(src_ref=src, dst_ref=src, send_sem=sem, recv_sem=b_recv.at[0],
                                     device_id=x_dev, device_id_type=MESH).wait_send()

    @pl.when(diag)
    def _():
        sent(t_ref, y_send)
        sent(z_ref.at[pl.ds(0, half - extra)], f_send)
        sent(a_ref, x_send)

    @pl.when(far)
    def _():
        sent(a_ref.at[pl.ds(0, half)], y_send)
        sent(z_ref.at[pl.ds(half, half)], f_send)
        sent(t_ref, x_send)

    def done_b(i, carry):
        give_b(i).wait_send()
        return carry
    lax.fori_loop(0, own, done_b, 0)
    for q in range(4):
        give_c(q).wait_send()


def solution(mesh, extra=EXTRA, tile=256, out_tile=768):
    grid_spec = P(("dp", "ri", "ro"), "co")

    def local_block(a_block, b_block):
        m, k = a_block.shape
        depth, n = b_block.shape
        half, kt = m // 2, k // PIECES
        bf16, f32 = jnp.bfloat16, jnp.float32
        hbm = pl.BlockSpec(memory_space=pl.ANY)
        dma = pltpu.SemaphoreType.DMA
        outs = pl.pallas_call(
            functools.partial(_kernel, extra, tile, out_tile),
            out_shape=[
                jax.ShapeDtypeStruct((m, n), bf16),
                jax.ShapeDtypeStruct((m, k), bf16),
                jax.ShapeDtypeStruct((m, k), bf16),
                jax.ShapeDtypeStruct((half + extra, k), bf16),
                jax.ShapeDtypeStruct((depth, n), bf16),
                jax.ShapeDtypeStruct((m, n), f32),
                jax.ShapeDtypeStruct((m, n), f32),
            ],
            in_specs=[hbm, hbm],
            out_specs=[hbm] * 7,
            scratch_shapes=[
                pltpu.VMEM((half, n), f32),
                pltpu.VMEM((half // 2, n), f32),
                pltpu.VMEM((2, half, kt), bf16),
                pltpu.VMEM((2, kt, n), bf16),
                pltpu.VMEM((2, half, out_tile), f32),
                pltpu.VMEM((2, half, out_tile), bf16),
                dma((2, PIECES)), dma((2, PIECES)), dma((2, PIECES)), dma((2 * PIECES,)),
                dma((PIECES // 2,)), dma((4,)),
                dma, dma, dma, dma((PIECES // 2,)), dma((4,)),
                dma((2,)), dma((2,)), dma, dma((2,)), dma((2,)),
            ],
            compiler_params=pltpu.CompilerParams(
                collective_id=0, has_side_effects=True, vmem_limit_bytes=66_000_000),
        )(a_block, b_block)
        return outs[0]

    return jax.shard_map(local_block, mesh=mesh, in_specs=(grid_spec, grid_spec), out_specs=grid_spec, check_vma=False)
```

time: 4160 us -> 1660 us (0.40)
  waiting for transfers between devices: 3540 us -> 0 us
  Pallas kernels: 0 us -> 1620 us
  matrix products: 605 us -> 0 us
    all_gather x2 -> x0, waiting for transfers between devices: 3540 us -> none  [the longest x1 2580 us: local_block(): b_cols = lax.all_gather(b_block, ('ri', 'ro'), axis=0, tiled=True)]
    pallas_call x0 -> x1, Pallas kernels: none -> 1620 us  [local_block(): pl.pallas_call(functools.partial(_kernel, extra, tile, out_tile), out_sha...]
    dot_general x1 -> x0, matrix products: 605 us -> none  [local_block(): product = jnp.dot(a_rows, b_cols, preferred_element_type=jnp.float32)]
  transfers between devices with their start and end apart: 2 -> 0, of which waited for: 2 -> 0; matrix products, arithmetic and copies ran while one was open for 0% -> 0% of each run, Pallas kernels for 0% -> 0%
where the time goes in v2:
time: 1660 us; the launch traced here: 1640 us
  Pallas kernels  1620 us (98%)
    pallas_call x1, Pallas kernels, local_block(): pl.pallas_call(functools.partial(_kernel, extra, tile, out_tile), out_sha...  1620 us

profile of v2, /device:TPU:0, one launch (start us, length us, event | category | flops | bytes accessed | tf_op | source)
XLA Modules:
  0.0 1640.3 jit_solution(2001990353943775831)
XLA Ops:
  0.0 1624.5 %shard_map.28 = (bf16[1280,6912]{1,0:T(8,128)(2,1)}, bf16[1280,16384]{1,0:T(8,128)(2,1)}, bf16[1280,16384]{1,0:T(8,128)(2,1)}, bf16[720,16384]{1,0:T(8,128)(2,1)...) custom-call(bf16[1280,16384]{1,0:T(8,128)(2,1)} %a_ref.1, bf16[8192,6912]{1,0:T(8,128)(2,1)} %b_ref.1), custom_call_target="tpu_custom_call" | custom-call | tf_op jit(solution)/shard_map/pallas_call | solution.py:359
  1624.5 15.7 copy.4

commit v3 on v2

--- a/solution.py
+++ b/solution.py
@@ -10,7 +10,7 @@
 MESH = pl.DeviceIdType.MESH
 PIECES = 16
 EXTRA = 80
-AHEAD = 8
+B_PARTS = 4
 
 
 def _kernel(extra, tile, out_tile, a_ref, b_ref, c_ref, z_ref, x_ref, t_ref, bs_ref, ps_ref, pr_ref,
@@ -89,22 +89,28 @@
         n = quart if r.size == quart else half
         return pltpu.make_async_copy(src.at[r, kcols(j)], av.at[slot, pl.ds(0, n)], a_sem.at[slot])
 
+    def load_b(src, i, slot):
+        n = kt // B_PARTS
+        for p in range(B_PARTS):
+            pltpu.make_async_copy(src.at[rows(i * kt + p * n, n)], bv.at[slot, pl.ds(p * n, n)], b_sem.at[slot]).start()
+
     def start_b(j, fresh=False):
         slot = lax.rem(j, 2)
 
         @pl.when(j < own)
         def _():
-            pltpu.make_async_copy(b_ref.at[rows(j * kt, kt)], bv.at[slot], b_sem.at[slot]).start()
+            load_b(b_ref, j, slot)
 
         @pl.when(j >= own)
         def _():
             if fresh:
                 give_b(j - own).wait_recv()
-            pltpu.make_async_copy(bs_ref.at[rows((j - own) * kt, kt)], bv.at[slot], b_sem.at[slot]).start()
+            load_b(bs_ref, j - own, slot)
 
     def wait_b(j):
         slot = lax.rem(j, 2)
-        pltpu.make_async_copy(b_ref.at[rows(0, kt)], bv.at[slot], b_sem.at[slot]).wait()
+        with jax.named_scope("wait_b"):
+            pltpu.make_async_copy(b_ref.at[rows(0, kt)], bv.at[slot], b_sem.at[slot]).wait()
 
     def next_b(j, fresh=False, last=False):
         if last:
@@ -115,27 +121,33 @@
             start_b(lax.rem(j + 1, PIECES), fresh)
 
     def multiply(total, n, j):
+        with jax.named_scope("mul"):
+            multiply_in(total, n, j)
+
+    def multiply_in(total, n, j):
         slot = lax.rem(j, 2)
-
-        def product(i):
-            cs = pl.ds(pl.multiple_of(i * tile, tile), tile)
-            return cs, jnp.dot(av[slot, :n], bv[slot, :, cs], preferred_element_type=jnp.float32)
+        wide = out_tile // tile
+
+        def products(i):
+            for t in range(wide):
+                cs = pl.ds(pl.multiple_of(i * out_tile + t * tile, tile), tile)
+                yield cs, jnp.dot(av[slot, :n], bv[slot, :, cs], preferred_element_type=jnp.float32)
 
         @pl.when(j == 0)
         def _():
             def body(i, carry):
-                cs, part = product(i)
-                total[:, cs] = part
+                for cs, part in products(i):
+                    total[:, cs] = part
                 return carry
-            lax.fori_loop(0, cols // tile, body, 0)
+            lax.fori_loop(0, cols // out_tile, body, 0)
 
         @pl.when(j > 0)
         def _():
             def body(i, carry):
-                cs, part = product(i)
-                total[:, cs] += part
+                for cs, part in products(i):
+                    total[:, cs] += part
                 return carry
-            lax.fori_loop(0, cols // tile, body, 0)
+            lax.fori_loop(0, cols // out_tile, body, 0)
 
     def store_total(r):
         store = pltpu.make_async_copy(zacc, ps_ref.at[r], p_sem)
@@ -195,6 +207,10 @@
             def go(j, carry):
                 first_x(h, j).start()
                 first_y(h, j).start()
+                if h == 0:
+                    @pl.when(lax.rem(j, 2) == 0)
+                    def _():
+                        give_b(j // 2).start()
                 return carry
             lax.fori_loop(0, PIECES, go, 0)
 
@@ -204,24 +220,21 @@
 
     @pl.when(diag)
     def _():
-        lax.fori_loop(0, AHEAD, go_x, 0)
-
-    def go_b(i, carry):
-        give_b(i).start()
-        return carry
-    lax.fori_loop(0, own, go_b, 0)
+        def go(i, carry):
+            give_x(i).start()
+            give_b(i).start()
+            return carry
+        lax.fori_loop(0, own, go, 0)
     start_b(0)
 
     for h in range(2):
         def f_step(j, carry):
-            next_b(j, fresh=h == 0)
-
             @pl.when(diag)
             def _():
                 with jax.named_scope("wait_zf_diag"):
                     first_y(h, j).wait_recv()
+                load_a(z_ref, f_rows(h), j).start()
                 pass_diag(h, j).start()
-                load_a(z_ref, f_rows(h), j).start()
                 with jax.named_scope("wait_t"):
                     first_x(h, j).wait_recv()
                 relay(h, j).start()
@@ -230,11 +243,11 @@
             def _():
                 with jax.named_scope("wait_zf_far"):
                     relay(h, j).wait_recv()
+                load_a(z_ref, f_rows(h), j).start()
                 pass_far(h, j).start()
-                load_a(z_ref, f_rows(h), j).start()
+            next_b(j, fresh=h == 0)
             load_a(z_ref, f_rows(h), j).wait()
-            with jax.named_scope("wait_b"):
-                wait_b(j)
+            wait_b(j)
             multiply(zacc, quart, j)
             return carry
         lax.fori_loop(0, PIECES, f_step, 0)
@@ -242,7 +255,7 @@
         if h == 1:
             @pl.when(diag)
             def _():
-                lax.fori_loop(AHEAD, 2 * PIECES, go_x, 0)
+                lax.fori_loop(own, 2 * PIECES, go_x, 0)
         store_total(f_rows(h))
     give_c(0).start()
     give_c(1).start()
@@ -250,14 +263,26 @@
     def x_block(blk, base, diag_branch, last):
         src = a_ref if diag_branch else x_ref
 
-        def x_step(j, carry):
-            next_b(j, last=last)
-            if diag_branch:
-                load_a(src, rows(base, half), j).start()
-            else:
+        def bring(j):
+            if not diag_branch:
                 with jax.named_scope("wait_x"):
                     give_x(blk * PIECES + j).wait_recv()
-                load_a(src, rows(base, half), j).start()
+            load_a(src, rows(base, half), j).start()
+
+        late = last and not diag_branch
+        ahead = PIECES - 1 if late else PIECES
+        bring(0)
+
+        def x_step(j, carry):
+            if late:
+                @pl.when(j == PIECES - 1)
+                def _():
+                    bring(j)
+
+            @pl.when(j + 1 < ahead)
+            def _():
+                bring(j + 1)
+            next_b(j, last=last)
             load_a(src, rows(base, half), j).wait()
             wait_b(j)
 
@@ -276,9 +301,7 @@
             x_block(0, g, True, False)
 
     for h in range(2):
-        def g_step(j, carry):
-            next_b(j)
-
+        def bring_z(j):
             @pl.when(diag)
             def _():
                 with jax.named_scope("wait_zg_diag"):
@@ -289,6 +312,13 @@
                 with jax.named_scope("wait_zg_far"):
                     pass_diag(h, j).wait_recv()
             load_a(z_ref, g_rows(h), j).start()
+        bring_z(0)
+
+        def g_step(j, carry):
+            @pl.when(j + 1 < PIECES)
+            def _():
+                bring_z(j + 1)
+            next_b(j)
             load_a(z_ref, g_rows(h), j).wait()
             wait_b(j)
             multiply(zacc, quart, j)

time: 1660 us -> 1330 us (0.80); the launches traced: 1640 us -> 1330 us
  Pallas kernels: 1620 us -> 1320 us
    pallas_call x1, Pallas kernels: 1620 us -> 1320 us  [local_block(): pl.pallas_call(functools.partial(_kernel, extra, tile, out_tile), out_sha...]
where the time goes in v3:
time: 1330 us
  Pallas kernels  1320 us (99%)
  local copies, waits for them, and re-layouts  15.7 us (1%)
    pallas_call x1, Pallas kernels, local_block(): pl.pallas_call(functools.partial(_kernel, extra, tile, out_tile), out_sha...  1320 us

profile of v3, /device:TPU:0, one launch (start us, length us, event | category | flops | bytes accessed | tf_op | source)
XLA Modules:
  0.0 1331.9 jit_solution(9037952768736714469)
XLA Ops:
  0.0 1316.1 %shard_map.28 = (bf16[1280,6912]{1,0:T(8,128)(2,1)}, bf16[1280,16384]{1,0:T(8,128)(2,1)}, bf16[1280,16384]{1,0:T(8,128)(2,1)}, bf16[720,16384]{1,0:T(8,128)(2,1)...) custom-call(bf16[1280,16384]{1,0:T(8,128)(2,1)} %a_ref.1, bf16[8192,6912]{1,0:T(8,128)(2,1)} %b_ref.1), custom_call_target="tpu_custom_call" | custom-call | tf_op jit(solution)/shard_map/pallas_call | solution.py:389
  1316.1 15.7 %copy.4 = bf16[1280,6912]{1,0:T(8,128)(2,1)} copy(bf16[1280,6912]{1,0:T(8,128)(2,1)} %get-tuple-element.6) | data formatting | bytes 35389440

commit v4 on v3

--- a/solution.py
+++ b/solution.py
@@ -9,7 +9,7 @@
 
 MESH = pl.DeviceIdType.MESH
 PIECES = 16
-EXTRA = 80
+EXTRA = 88
 B_PARTS = 4
 
 
@@ -76,6 +76,10 @@
         at = (rows(q // PIECES * half, half), kcols(lax.rem(q, PIECES)))
         return remote(a_ref.at[at], x_ref.at[at], x_send, x_recv.at[q], x_dev)
 
+    def give_last(h):
+        at = (pl.ds((3 - h) * quart, quart), kcols(PIECES - 1))
+        return remote(a_ref.at[at], x_ref.at[at], x_send, x_recv.at[2 * PIECES - 1 + h], x_dev)
+
     def give_b(i):
         r = rows(i * kt, kt)
         return remote(b_ref.at[r], bs_ref.at[r], b_send.at[i], b_recv.at[i], sib)
@@ -112,13 +116,8 @@
         with jax.named_scope("wait_b"):
             pltpu.make_async_copy(b_ref.at[rows(0, kt)], bv.at[slot], b_sem.at[slot]).wait()
 
-    def next_b(j, fresh=False, last=False):
-        if last:
-            @pl.when(j + 1 < PIECES)
-            def _():
-                start_b(j + 1)
-        else:
-            start_b(lax.rem(j + 1, PIECES), fresh)
+    def next_b(j, fresh=False):
+        start_b(lax.rem(j + 1, PIECES), fresh)
 
     def multiply(total, n, j):
         with jax.named_scope("mul"):
@@ -156,17 +155,19 @@
 
     n_out = cols // out_tile
 
-    def finish(base, from_step):
+    def finish(r, at_row, n_rows, piece_row=None):
+        tall = pl.ds(0, n_rows)
+
         def part(n):
             return pl.ds(pl.multiple_of(n * out_tile, out_tile), out_tile)
 
         def fetch(n):
             at = lax.rem(n, 2)
-            return pltpu.make_async_copy(pr_ref.at[rows(base, half), part(n)], prv.at[at], pr_sem.at[at])
+            return pltpu.make_async_copy(pr_ref.at[r, part(n)], prv.at[at, tall], pr_sem.at[at])
 
         def put(n):
             at = lax.rem(n, 2)
-            return pltpu.make_async_copy(ov.at[at], c_ref.at[rows(base, half), part(n)], o_sem.at[at])
+            return pltpu.make_async_copy(ov.at[at, tall], c_ref.at[r, part(n)], o_sem.at[at])
 
         fetch(0).start()
 
@@ -184,17 +185,39 @@
             for i in range(out_tile // tile):
                 ts = pl.ds(i * tile, tile)
                 cs = pl.ds(pl.multiple_of(n * out_tile + i * tile, tile), tile)
-                total = acc[:, cs] + prv[at, :, ts]
-                if from_step:
-                    total += jnp.dot(av[(PIECES - 1) % 2], bv[(PIECES - 1) % 2, :, cs],
+                total = acc[pl.ds(at_row, n_rows), cs] + prv[at, :n_rows, ts]
+                if piece_row is not None:
+                    slot = (PIECES - 1) % 2
+                    total += jnp.dot(av[slot, piece_row:piece_row + n_rows], bv[slot, :, cs],
                                      preferred_element_type=jnp.float32)
-                ov[at, :, ts] = total.astype(ov.dtype)
+                ov[at, :n_rows, ts] = total.astype(ov.dtype)
             put(n).start()
             return carry
         lax.fori_loop(0, n_out, body, 0)
         if n_out >= 2:
             put(n_out - 2).wait()
         put(n_out - 1).wait()
+
+    def finish_last():
+        wait_b(PIECES - 1)
+        slot = (PIECES - 1) % 2
+        for h in range(2):
+            def bring(src):
+                return pltpu.make_async_copy(src.at[f_rows(h), kcols(PIECES - 1)],
+                                             av.at[slot, pl.ds(h * quart, quart)], a_sem.at[slot])
+
+            @pl.when(diag)
+            def _():
+                bring(a_ref).start()
+
+            @pl.when(far)
+            def _():
+                give_last(h).wait_recv()
+                bring(x_ref).start()
+            give_c(2 + h).wait_recv()
+            bring(a_ref).wait()
+            at_row = pl.multiple_of(jnp.where(diag, h, 1 - h) * quart, 8)
+            finish(f_rows(h), at_row, quart, h * quart)
 
     barrier = pltpu.get_barrier_semaphore()
     for dev in (x_dev, y_dev, sib):
@@ -255,7 +278,9 @@
         if h == 1:
             @pl.when(diag)
             def _():
-                lax.fori_loop(own, 2 * PIECES, go_x, 0)
+                lax.fori_loop(own, 2 * PIECES - 1, go_x, 0)
+                give_last(0).start()
+                give_last(1).start()
         store_total(f_rows(h))
     give_c(0).start()
     give_c(1).start()
@@ -269,31 +294,19 @@
                     give_x(blk * PIECES + j).wait_recv()
             load_a(src, rows(base, half), j).start()
 
-        late = last and not diag_branch
-        ahead = PIECES - 1 if late else PIECES
+        count = PIECES - 1 if last else PIECES
         bring(0)
 
         def x_step(j, carry):
-            if late:
-                @pl.when(j == PIECES - 1)
-                def _():
-                    bring(j)
-
-            @pl.when(j + 1 < ahead)
+            @pl.when(j + 1 < count)
             def _():
                 bring(j + 1)
-            next_b(j, last=last)
+            next_b(j)
             load_a(src, rows(base, half), j).wait()
             wait_b(j)
-
-            if last:
-                @pl.when(j < PIECES - 1)
-                def _():
-                    multiply(acc, half, j)
-            else:
-                multiply(acc, half, j)
+            multiply(acc, half, j)
             return carry
-        lax.fori_loop(0, PIECES, x_step, 0)
+        lax.fori_loop(0, count, x_step, 0)
 
     @pl.when(diag)
     def _():
@@ -336,7 +349,7 @@
         give_c(0).wait_recv()
         give_c(1).wait_recv()
     with jax.named_scope("finish_first"):
-        finish(g, False)
+        finish(rows(g, half), 0, half)
 
     @pl.when(diag)
     def _():
@@ -346,11 +359,7 @@
     def _():
         x_block(1, f, False, True)
 
-    with jax.named_scope("wait_c_last"):
-        give_c(2).wait_recv()
-        give_c(3).wait_recv()
-    with jax.named_scope("finish_last"):
-        finish(f, True)
+    finish_last()
 
     def sent(src, sem):
         pltpu.make_async_remote_copy(src_ref=src, dst_ref=src, send_sem=sem, recv_sem=b_recv.at[0],
@@ -406,7 +415,7 @@
                 pltpu.VMEM((2, kt, n), bf16),
                 pltpu.VMEM((2, half, out_tile), f32),
                 pltpu.VMEM((2, half, out_tile), bf16),
-                dma((2, PIECES)), dma((2, PIECES)), dma((2, PIECES)), dma((2 * PIECES,)),
+                dma((2, PIECES)), dma((2, PIECES)), dma((2, PIECES)), dma((2 * PIECES + 1,)),
                 dma((PIECES // 2,)), dma((4,)),
                 dma, dma, dma, dma((PIECES // 2,)), dma((4,)),
                 dma((2,)), dma((2,)), dma, dma((2,)), dma((2,)),

time: 1330 us -> 1330 us (level)
  no operation moved by 1% of the time
where the time goes in v4:
time: 1330 us
  Pallas kernels  1320 us (99%)
  local copies, waits for them, and re-layouts  15.7 us (1%)
    pallas_call x1, Pallas kernels, local_block(): pl.pallas_call(functools.partial(_kernel, extra, tile, out_tile), out_sha...  1320 us

profile of v4, /device:TPU:0, one launch (start us, length us, event | category | flops | bytes accessed | tf_op | source)
XLA Modules:
  0.0 1332.6 jit_solution(9400743955495652093)
XLA Ops:
  0.0 1316.8 %shard_map.28 = (bf16[1280,6912]{1,0:T(8,128)(2,1)}, bf16[1280,16384]{1,0:T(8,128)(2,1)}, bf16[1280,16384]{1,0:T(8,128)(2,1)}, bf16[728,16384]{1,0:T(8,128)(2,1)...) custom-call(bf16[1280,16384]{1,0:T(8,128)(2,1)} %a_ref.1, bf16[8192,6912]{1,0:T(8,128)(2,1)} %b_ref.1), custom_call_target="tpu_custom_call" | custom-call | tf_op jit(solution)/shard_map/pallas_call | solution.py:398
  1316.9 15.7 %copy.4 = bf16[1280,6912]{1,0:T(8,128)(2,1)} copy(bf16[1280,6912]{1,0:T(8,128)(2,1)} %get-tuple-element.6) | data formatting | bytes 35389440
